TPU v7x, 256 devices: a whole 4x4x8 slice. The times are simulated.
256 devices in a mesh: dp: 8 (over y, core), expert: 8 (over z), tile: 4 (over x).
Axes of the slice: x: 4, y: 4, z: 8, core: 2. Of those that a mesh axis runs over, the one named last changes fastest.
Arguments:
- tokens: bfloat16 [4096, 4096], P(('dp', 'expert'), 'tile'), may hold values from -6 to 6
- hidden: bfloat16 [4096, 2, 7168], P(('dp', 'expert'), None, 'tile'), may hold values from -6 to 6
- routes: int32 [4096, 2], P(('dp', 'expert')), may hold values from 0 to 7, all different within a row; in each aligned block of 64 rows (0 to 63, 64 to 127, ...) at most 24 rows name the same one
- lengths: int32 [64], P(('dp', 'expert')), may hold values from 1 to 64, as said below
Outputs:
- hessian_in: float32 [8, 4096, 4096], P('expert', 'tile', 'dp')
- hessian_down: float32 [8, 7168, 7168], P('expert', 'tile', 'dp')
Inputs may be any that keep to these rules, and one draw needn't show every extreme that they name: `routes`: in each aligned block of 64 rows (the rows of one group) no expert is named by more than 24 rows, a bound that some block reaches. The live rows of group g are its first lengths[g] rows; the last group is full.
All inputs are finite; a program needn't handle non-finite values.
Results may differ from a plain program's by a relative error of at most 0.0003.
Values may be sent and summed in bfloat16 or wider, within the bound.
A program may use at most 64 MiB of HBM per device.

v0:
```python
import jax
import jax.numpy as jnp
from jax import lax
from jax.sharding import PartitionSpec as P


def sent_together(arrays, axis, split_dim, concat_dim, along):
    widths = [a.shape[along] for a in arrays]
    both = jnp.concatenate(arrays, axis=along)
    out = lax.all_to_all(both, axis, split_axis=split_dim, concat_axis=concat_dim, tiled=True)
    return tuple(jnp.split(out, [sum(widths[:k]) for k in range(1, len(widths))], axis=along))


def from_everyone(value, axis):
    copies = jnp.broadcast_to(value, (lax.axis_size(axis), *value.shape))
    return lax.all_to_all(copies, axis, split_axis=0, concat_axis=0, tiled=True)


def of_everyone(value, axis):
    everything = from_everyone(value, axis)
    return jnp.sum(everything, axis=0)


def side_by_side(arrays, axis, dim, along):
    ends, at = ([], 0)
    for a in arrays[:-1]:
        at += a.shape[along]
        ends.append(at)
    both = jnp.concatenate(arrays, axis=along)
    return tuple(jnp.split(lax.all_gather(both, axis, axis=dim, tiled=True), ends, axis=along))


def contract(left, right):
    return lax.dot_general(
        left, right, (((0,), (0,)), ((), ())), preferred_element_type=jnp.float32
    )


def dispatch_tables(routes, live_count, experts, share_size, senders):
    token_count = routes.shape[0]
    top_count = routes.shape[1]
    flat_routes = routes.reshape(token_count * top_count)
    pair_index = jnp.arange(token_count * top_count, dtype=jnp.int32)
    pair_live = pair_index // top_count < live_count
    expert_ids = jnp.arange(experts, dtype=jnp.int32)
    onehot = ((flat_routes[:, None] == expert_ids[None, :]) & pair_live[:, None]).astype(
        jnp.float32
    )
    before = jnp.cumsum(onehot, axis=0) - onehot
    position = jnp.sum(before * onehot, axis=1).astype(jnp.int32)
    target = (
        position // share_size * (experts * share_size)
        + flat_routes * share_size
        + position % share_size
    )
    slot_total = senders * experts * share_size
    placed = (target[None, :] == jnp.arange(slot_total, dtype=jnp.int32)[:, None]) & pair_live[
        None, :
    ]
    return (placed.astype(jnp.float32), jnp.sum(onehot, axis=0))


def on_device(tokens, hidden, routes, lengths):
    experts = lax.axis_size("expert")
    senders = lax.axis_size("dp")
    token_count = tokens.shape[0]
    top_count = routes.shape[1]
    share_size = (5 * token_count + 2 * experts * senders - 1) // (2 * experts * senders)
    placed, local_counts = dispatch_tables(routes, lengths[0], experts, share_size, senders)
    slot_total = placed.shape[0]
    by_token = jnp.sum(placed.reshape(slot_total, token_count, top_count), axis=2).astype(
        jnp.bfloat16
    )
    send_tokens = jnp.dot(by_token, tokens, preferred_element_type=jnp.float32).astype(jnp.bfloat16)
    flat_hidden = hidden.reshape(token_count * top_count, hidden.shape[2])
    send_hidden = jnp.dot(
        placed.astype(jnp.bfloat16), flat_hidden, preferred_element_type=jnp.float32
    ).astype(jnp.bfloat16)
    slot_tokens, slot_hidden = sent_together((send_tokens, send_hidden), ("dp", "expert"), 0, 0, 1)
    global_counts = of_everyone(local_counts, ("dp", "expert"))
    own_expert = lax.axis_index("expert")
    own_count = jnp.sum(
        jnp.where(jnp.arange(experts, dtype=jnp.int32) == own_expert, global_counts, 0.0)
    )
    factor = 2.0 / jnp.maximum(own_count, 1.0)
    full_tokens, full_hidden = (
        lax.all_gather(slot_tokens, "tile", axis=1, tiled=True),
        lax.all_gather(slot_hidden, "tile", axis=1, tiled=True),
    )
    column_tokens, column_hidden = (
        lax.all_to_all(full_tokens, "dp", split_axis=1, concat_axis=0, tiled=True),
        lax.all_to_all(full_hidden, "dp", split_axis=1, concat_axis=0, tiled=True),
    )
    pieces = side_by_side((slot_tokens, slot_hidden), "dp", 0, 1)
    gram_tokens = contract(pieces[0], column_tokens)
    gram_hidden = contract(pieces[1], column_hidden)
    return ((gram_tokens * factor)[None], (gram_hidden * factor)[None])


def solution(mesh):
    placed = (
        P(("dp", "expert"), "tile"),
        P(("dp", "expert"), None, "tile"),
        P(("dp", "expert"), None),
        P(("dp", "expert")),
    )
    return jax.shard_map(
        on_device,
        mesh=mesh,
        in_specs=placed,
        out_specs=(P("expert", "tile", "dp"), P("expert", "tile", "dp")),
        check_vma=False,
    )
```

profile of v0, /device:TPU:8, one launch (start us, length us, event | category | flops | bytes accessed | tf_op | source)
XLA Modules:
  0.0 224.1 jit_solution(10405702550066354825)
XLA Ops:
  7.2 0.0 copy-start
  7.2 0.0 all-gather.8.cloned.1.call-start
  7.9 0.8 copy.33
  8.7 0.1 eq.43
  8.8 0.1 fusion.11
  8.9 0.2 reduce_window_sum.11
  9.1 0.2 fusion.12
  9.3 0.1 rem.32
  9.5 0.1 copy.34
  9.5 0.1 div.25
  9.7 0.1 copy.36
  9.8 0.2 ne.82
  9.9 0.1 copy.35
  10.1 1.2 reshape.98
  11.2 0.7 fusion.18
  11.9 0.1 convert_reduce_fusion
  12.1 0.0 copy-done
  12.1 0.3 convolution_convert_fusion.1
  12.3 0.3 convolution_convert_fusion
  12.7 0.1 pad_maximum_fusion
  12.8 0.5 all_to_all.40
  13.3 48.6 %all_to_all.56 = bf16[64,3,2816]{2,1,0:T(4,128)(2,1)S(1)} all-to-all(bf16[64,3,2816]{2,1,0:T(4,128)(2,1)S(1)} %all_to_all.40), channel_id=1, replica_groups=mesh['dp'=8,'expert'=8,'tile'=4] {'dp','expert'}, dimensions={0} | all-to-all | bytes 2162688 | tf_op jit(solution)/shard_map/all_to_all | solution.py:10
  61.9 0.9 all_to_all.42
  62.8 0.0 copy-start.1
  62.8 1.0 split.19
  63.8 0.0 all-gather.8.cloned.1.call-update
  63.8 0.0 all-gather.6.cloned.1.call-start
  63.9 0.8 split.17
  64.7 0.0 all-gather.6.cloned.1.call-update
  64.7 0.0 all-gather.4.cloned.1.call-start
  64.7 0.0 copy-done.1
  64.8 0.7 all-gather.4.cloned.1.call-update
  65.4 0.6 broadcast_in_dim.18
  66.1 6.7 %all-to-all-start.2 = ((f32[64,1,8]{2,1,0:T(1,128)}), f32[64,1,8]{2,1,0:T(1,128)S(1)}, u32[]{:S(2)}, u32[]{:S(2)}) async-start(f32[64,1,8]{2,1,0:T(1,128)} %broadcast_in_dim.18), calls=%async_computation.2 | async-start | bytes 65536 | tf_op jit(solution)/shard_map/all_to_all | solution.py:16
  72.7 27.4 %all-gather.8.cloned.1.call-done = bf16[192,7168]{1,0:T(8,128)(2,1)} async-done(((bf16[192,1792]{1,0:T(8,128)(2,1)}), bf16[192,7168]{1,0:T(8,128)(2,1)}) %all-gather.8.cloned.1.call-update) | async-done | bytes 2752528 | tf_op jit(solution)/shard_map/all_gather | solution.py:88
  100.1 3.7 %copy.49 = bf16[24,8,8,896]{3,2,0,1:T(8,128)(2,1)} copy(bf16[24,8,8,896]{3,2,1,0:T(8,128)(2,1)} %bitcast.27) | data formatting | bytes 5505024 | tf_op jit(solution)/shard_map/all_to_all | solution.py:92
  103.8 0.0 all-to-all-done.2
  103.8 4.8 %all-to-all-start.3 = ((bf16[192,8,896]{2,0,1:T(8,128)(2,1)}), bf16[192,8,896]{2,0,1:T(8,128)(2,1)S(1)}, u32[]{:S(2)}, u32[]{:S(2)}) async-start(bf16[192,8,896]{2,0,1:T(8,128)(2,1)} %bitcast.22), calls=%async_computation.3 | async-start | bytes 5505024 | tf_op jit(solution)/shard_map/all_to_all | solution.py:92
  108.7 22.5 %all-gather.6.cloned.1.call-done = bf16[192,4096]{1,0:T(8,128)(2,1)} async-done(((bf16[192,1024]{1,0:T(8,128)(2,1)}), bf16[192,4096]{1,0:T(8,128)(2,1)}) %all-gather.6.cloned.1.call-update) | async-done | bytes 1572880 | tf_op jit(solution)/shard_map/all_gather | solution.py:87
  131.1 2.7 %copy.50 = bf16[24,8,8,512]{3,2,0,1:T(8,128)(2,1)} copy(bf16[24,8,8,512]{3,2,1,0:T(8,128)(2,1)} %bitcast.28) | data formatting | bytes 3145728 | tf_op jit(solution)/shard_map/all_to_all | solution.py:91
  133.8 7.6 %all-to-all-done.3 = bf16[192,8,896]{2,0,1:T(8,128)(2,1)S(1)} async-done(((bf16[192,8,896]{2,0,1:T(8,128)(2,1)}), bf16[192,8,896]{2,0,1:T(8,128)(2,1)S(1)}, u32[]{:S(2)}, u32[]{:S(2)}) %all-to-all-start.3) | async-done | bytes 2752544 | tf_op jit(solution)/shard_map/all_to_all | solution.py:92
  141.4 5.7 %all-to-all-start.1 = ((bf16[192,8,512]{2,0,1:T(8,128)(2,1)}), bf16[192,8,512]{2,0,1:T(8,128)(2,1)}, u32[]{:S(2)}, u32[]{:S(2)}) async-start(bf16[192,8,512]{2,0,1:T(8,128)(2,1)} %bitcast.23), calls=%async_computation.1 | async-start | bytes 3145728 | tf_op jit(solution)/shard_map/all_to_all | solution.py:91
  147.1 0.1 reduce_sum.48
  147.1 0.6 fusion.22
  148.4 54.0 %all-gather.4.cloned.1.call-done = bf16[1536,2816]{1,0:T(8,128)(2,1)} async-done(((bf16[192,2816]{1,0:T(8,128)(2,1)}), bf16[1536,2816]{1,0:T(8,128)(2,1)}) %all-gather.4.cloned.1.call-update) | async-done | bytes 8650768 | tf_op jit(solution)/shard_map/all_gather | solution.py:30
  202.4 9.6 %multiply_bitcast_fusion = f32[1,1792,896]{2,1,0:T(8,128)} fusion(bf16[1536,896]{1,0:T(8,128)(2,1)S(1)} %bitcast.26, bf16[1536,2816]{1,0:T(8,128)(2,1)} %all-gather.4.cloned.1.call-done, f32[]{:T(128)S(6)} %div.27), kind=kOutput, calls=%fused_computation | convolution fusion | flops 4934107136 | bytes 14680068 | tf_op jit(solution)/shard_map/dot_general | solution.py:34
  212.0 0.0 all-to-all-done.1
  212.0 5.5 %multiply_bitcast_fusion.1 = f32[1,1024,512]{2,1,0:T(8,128)} fusion(bf16[1536,512]{1,0:T(8,128)(2,1)} %bitcast.2, bf16[1536,2816]{1,0:T(8,128)(2,1)} %all-gather.4.cloned.1.call-done, f32[]{:T(128)S(6)} %div.27), kind=kOutput, calls=%fused_computation.7 | convolution fusion | flops 1611137024 | bytes 6815748 | tf_op jit(solution)/shard_map/dot_general | solution.py:34
  (4 shorter events, 0.1 us)
Async XLA Ops:
  7.2 4.9 %copy-start = (bf16[64,1024]{1,0:T(8,128)(2,1)S(1)}, bf16[64,1024]{1,0:T(8,128)(2,1)}, u32[]{:S(2)}) copy-start(bf16[64,1024]{1,0:T(8,128)(2,1)} %param.4) | copy-start | bytes 393220
  7.2 93.0 %all-gather.8.cloned.1.call-start = ((), (), s32[]{:S(2)}) async-start(), calls=%async_computation.6 | async-start | bytes 3440640 | tf_op jit(solution)/shard_map/all_gather | solution.py:88
  62.8 2.0 copy-start.1
  63.8 67.3 %all-gather.6.cloned.1.call-start = ((), (), s32[]{:S(2)}) async-start(), calls=%async_computation.5 | async-start | bytes 1966080 | tf_op jit(solution)/shard_map/all_gather | solution.py:87
  64.7 137.7 %all-gather.4.cloned.1.call-start = ((), (), s32[]{:S(2)}) async-start(), calls=%async_computation.4 | async-start | bytes 9732096 | tf_op jit(solution)/shard_map/all_gather | solution.py:30
  66.1 37.8 %all-to-all-start.2 = ((f32[64,1,8]{2,1,0:T(1,128)}), f32[64,1,8]{2,1,0:T(1,128)S(1)}, u32[]{:S(2)}, u32[]{:S(2)}) async-start(f32[64,1,8]{2,1,0:T(1,128)} %broadcast_in_dim.18), calls=%async_computation.2 | async-start | bytes 65536 | tf_op jit(solution)/shard_map/all_to_all | solution.py:16
  103.8 37.6 %all-to-all-start.3 = ((bf16[192,8,896]{2,0,1:T(8,128)(2,1)}), bf16[192,8,896]{2,0,1:T(8,128)(2,1)S(1)}, u32[]{:S(2)}, u32[]{:S(2)}) async-start(bf16[192,8,896]{2,0,1:T(8,128)(2,1)} %bitcast.22), calls=%async_computation.3 | async-start | bytes 5505024 | tf_op jit(solution)/shard_map/all_to_all | solution.py:92
  141.4 70.7 %all-to-all-start.1 = ((bf16[192,8,512]{2,0,1:T(8,128)(2,1)}), bf16[192,8,512]{2,0,1:T(8,128)(2,1)}, u32[]{:S(2)}, u32[]{:S(2)}) async-start(bf16[192,8,512]{2,0,1:T(8,128)(2,1)} %bitcast.23), calls=%async_computation.1 | async-start | bytes 3145728 | tf_op jit(solution)/shard_map/all_to_all | solution.py:91
Sparse Core Ops, SparseCore 0:
  63.9 36.1 all-gather.7
  102.0 29.1 all-gather.5
  133.0 69.3 all-gather.3
where the time goes:
time: 227 us; the launch traced here: 224 us
  waiting for transfers between devices  112 us (49%)
  blocking collectives  48.6 us (21%)
  starting transfers between devices  17.3 us (8%)
  matrix products  15.8 us (7%)
  between operations  15.3 us (7%)
  local copies, waits for them, and re-layouts  13 us (6%)
    all_gather x1, waiting for transfers between devices, side_by_side(): lax.all_gather(both, axis, axis=dim, tiled=True)  54 us
    all_to_all x1, blocking collectives, sent_together(): lax.all_to_all(both, axis, split_axis=split_dim, concat_axis=concat_dim,...  48.6 us
    all_gather x1, waiting for transfers between devices, on_device(): lax.all_gather(slot_hidden, 'tile', axis=1, tiled=True)  27.4 us
    all_gather x1, waiting for transfers between devices, on_device(): lax.all_gather(slot_tokens, 'tile', axis=1, tiled=True)  22.5 us
    dot_general x2, matrix products, contract(): lax.dot_general(left, right, (((0,), (0,)), ((), ())), preferred_element_...  15.2 us
    all_to_all x1, waiting for transfers between devices, on_device(): lax.all_to_all(full_hidden, 'dp', split_axis=1, concat_axis=0, tiled=True)  7.56 us
    all_to_all x1, starting transfers between devices, from_everyone(): return lax.all_to_all(copies, axis, split_axis=0, concat_axis=0, tiled=True)  6.67 us
    all_to_all x1, starting transfers between devices, on_device(): lax.all_to_all(full_tokens, 'dp', split_axis=1, concat_axis=0, tiled=True)  5.66 us
  transfers between devices with their start and end apart: 6, of which 4 were waited for; matrix products, arithmetic and copies ran while one was open for 8% of the time, Pallas kernels for 0%

commit v1 on v0

v1 whole, which is shorter than its diff:
```python
import functools

import jax
import jax.numpy as jnp
from jax import lax
from jax.experimental import pallas as pl
from jax.experimental.pallas import tpu as pltpu
from jax.sharding import PartitionSpec as P

MESH = pl.DeviceIdType.MESH
CAP = 24
ROWS = 2 * CAP


def positions(eff, experts, base):
    pairs = eff.shape[1]
    expert = lax.broadcasted_iota(jnp.int32, (experts, pairs), 0)
    hit = jnp.where(eff == expert, 1.0, 0.0)
    earlier = lax.broadcasted_iota(jnp.int32, (pairs, pairs), 0) < lax.broadcasted_iota(
        jnp.int32, (pairs, pairs), 1
    )
    before = jnp.dot(
        hit.astype(jnp.bfloat16),
        jnp.where(earlier, 1.0, 0.0).astype(jnp.bfloat16),
        preferred_element_type=jnp.float32,
    )
    rank = jnp.sum(hit * before, axis=0, keepdims=True).astype(jnp.int32)
    return eff * ROWS + base + rank


def exchange_kernel(
    nz, ny, nx,
    eff_ref, hid_ref, tok_ref,
    xh_out, xt_out, yh_out, yt_out, factor_out,
    eff_p, hid_p, tok_p, gath, xb, xo, yb, cs, cr, ys, yr,
    pair_s, pair_r, zs, zr, ysend, yrecv, xsend, xrecv, ds, dr, cz_s, cz_r, cy_s, cy_r, local_sem,
):
    d, z, x = lax.axis_index("dp"), lax.axis_index("expert"), lax.axis_index("tile")
    y, c = d // 2, d % 2
    wh = hid_ref.shape[1] // 2
    wt = tok_ref.shape[1] // 2

    def device(yy, cc, zz, xx):
        return {"dp": yy * 2 + cc, "expert": zz, "tile": xx}

    step = 1 - 2 * c
    y_next = lax.rem(y + step + ny, ny)
    x_next = lax.rem(x + step + nx, nx)
    place = lax.rem((x - y) * step + 2 * nx, nx)
    partner = device(y, 1 - c, z, x)
    to_y, to_x = device(y_next, c, z, x), device(y, c, z, x_next)

    def z_offset(k):
        return lax.rem(jnp.where(k % 2 == 1, (k + 1) // 2, nz - k // 2), nz)

    barrier = pltpu.get_barrier_semaphore()
    for o in range(1, nz):
        pl.semaphore_signal(barrier, inc=1, device_id=device(y, c, lax.rem(z + o, nz), x), device_id_type=MESH)
    for o in range(1, ny):
        pl.semaphore_signal(barrier, inc=1, device_id=device(lax.rem(y + o, ny), c, z, x), device_id_type=MESH)
    for o in (1, nx - 1):
        pl.semaphore_signal(barrier, inc=1, device_id=device(y, c, z, lax.rem(x + o, nx)), device_id_type=MESH)
    pl.semaphore_signal(barrier, inc=1, device_id=partner, device_id_type=MESH)
    pl.semaphore_wait(barrier, nz - 1 + ny - 1 + 2 + 1)

    def remote(src, dst, s, r, to):
        return pltpu.make_async_remote_copy(
            src_ref=src, dst_ref=dst, send_sem=s, recv_sem=r, device_id=to, device_id_type=MESH
        )

    theirs_h = pl.ds(pl.multiple_of((1 - c) * wh, 128), wh)
    theirs_t = pl.ds(pl.multiple_of((1 - c) * wt, 128), wt)
    swaps = (
        remote(eff_ref, eff_p, pair_s.at[0], pair_r.at[0], partner),
        remote(hid_ref.at[:, theirs_h], hid_p, pair_s.at[1], pair_r.at[1], partner),
        remote(tok_ref.at[:, theirs_t], tok_p, pair_s.at[2], pair_r.at[2], partner),
    )
    for s in swaps:
        s.start()
    eff_mine = eff_ref[...]
    mine_h = hid_ref[:, pl.ds(pl.multiple_of(c * wh, 128), wh)]
    mine_t = tok_ref[:, pl.ds(pl.multiple_of(c * wt, 128), wt)]
    mine_t2 = jnp.concatenate([mine_t, mine_t], axis=0)
    slot_mine = positions(eff_mine, nz, c * CAP)
    for s in swaps:
        s.wait_recv()
    eff_theirs = eff_p[...]
    slot_theirs = positions(eff_theirs, nz, (1 - c) * CAP)
    pairs = eff_mine.shape[1]

    def gathered(e, out):
        slot = lax.broadcasted_iota(jnp.int32, (ROWS, pairs), 0) + e * ROWS
        a = jnp.where(slot == slot_mine, 1.0, 0.0).astype(jnp.bfloat16)
        b = jnp.where(slot == slot_theirs, 1.0, 0.0).astype(jnp.bfloat16)
        their_t = tok_p[...]
        out[:, :wh] = (
            jnp.dot(a, mine_h, preferred_element_type=jnp.float32)
            + jnp.dot(b, hid_p[...], preferred_element_type=jnp.float32)
        ).astype(jnp.bfloat16)
        out[:, wh:] = (
            jnp.dot(a, mine_t2, preferred_element_type=jnp.float32)
            + jnp.dot(b, jnp.concatenate([their_t, their_t], axis=0), preferred_element_type=jnp.float32)
        ).astype(jnp.bfloat16)

    def tally(e):
        hits = jnp.where(eff_mine == e, 1.0, 0.0) + jnp.where(eff_theirs == e, 1.0, 0.0)
        return jnp.broadcast_to(jnp.sum(hits, axis=1, keepdims=True), (8, 128))

    gathered(z, xb.at[0, y])

    def z_copy(k):
        to = device(y, c, lax.rem(z + nz - z_offset(k), nz), x)
        return remote(gath.at[k], xb.at[k, y], zs.at[k], zr.at[k], to)

    def count_copy(k):
        to = device(y, c, lax.rem(z + nz - z_offset(k), nz), x)
        return remote(cs.at[k], cr.at[k], cz_s.at[k], cz_r.at[k], to)

    def fill(k, carry):
        e = lax.rem(z + nz - z_offset(k), nz)
        gathered(e, gath.at[k])
        cs[k] = tally(e)
        z_copy(k).start()
        count_copy(k).start()
        return carry

    lax.fori_loop(1, nz, fill, 0)

    def row_of(h):
        return lax.rem(y + ny * h - h * step, ny)

    def y_copy(k, h):
        yy = row_of(h)
        return remote(xb.at[k, yy], xb.at[k, yy], ysend.at[k, h], yrecv.at[k, h + 1], to_y)

    def y_arrival(k, h):
        yy = row_of(h)
        return remote(xb.at[k, yy], xb.at[k, yy], ysend.at[k, h - 1], yrecv.at[k, h], to_y)

    def x_first(k, h):
        yy = row_of(h)
        return remote(xb.at[k, yy], yb.at[k, yy], xsend.at[k, h], xrecv.at[k, h], to_x)

    def x_copy(k, h):
        yy = row_of(h)
        return remote(yb.at[k, yy], yb.at[k, yy], xsend.at[k, h], xrecv.at[k, h], to_x)

    def d_copy(k):
        return remote(xb.at[k], xo.at[k], ds.at[k], dr.at[k], partner)

    def outs_of(k, src, half, at):
        return (
            pltpu.make_async_copy(src.at[k, :, :, pl.ds(0, wh)], xh_out.at[half, k], local_sem.at[k, at]),
            pltpu.make_async_copy(src.at[k, :, :, pl.ds(wh, wt)], xt_out.at[half, k], local_sem.at[k, at + 1]),
        )

    def outs_y(k, src):
        return (
            pltpu.make_async_copy(src.at[k, :, :, pl.ds(0, wh)], yh_out.at[k], local_sem.at[k, 4]),
            pltpu.make_async_copy(src.at[k, :, :, pl.ds(wh, wt)], yt_out.at[k], local_sem.at[k, 5]),
        )

    def starts(copies):
        for copy in copies:
            copy.start()

    lag = place + 1

    def round_of(i, carry):
        @pl.when(i < nz)
        def _():
            @pl.when(i > 0)
            def _():
                z_copy(i).wait_recv()

            y_copy(i, 0).start()

            @pl.when(place == 0)
            def _():
                x_first(i, 0).start()

        for h in range(1, ny):
            k = i - h

            @pl.when((k >= 0) & (k < nz))
            def _():
                y_arrival(k, h).wait_recv()
                if h < ny - 1:
                    y_copy(k, h).start()

                @pl.when(place == 0)
                def _():
                    x_first(k, h).start()

                if h == ny - 1:
                    d_copy(k).start()
                    starts(outs_of(k, xb, c, 0))

                    @pl.when(place == 0)
                    def _():
                        starts(outs_y(k, xb))

        @pl.when(place > 0)
        def _():
            for h in range(ny):
                k = i - lag - h

                @pl.when((k >= 0) & (k < nz))
                def _():
                    x_first(k, h).wait_recv()

                    @pl.when(place < nx - 1)
                    def _():
                        x_copy(k, h).start()

                    if h == ny - 1:
                        starts(outs_y(k, yb))

        k_out = i - ny - 1

        @pl.when((k_out >= 0) & (k_out < nz))
        def _():
            d_copy(k_out).wait_recv()
            starts(outs_of(k_out, xo, 1 - c, 2))

        return carry

    lax.fori_loop(0, nz, round_of, 0)

    total = tally(z)
    for k in range(1, nz):
        count_copy(k).wait_recv()
        total = total + cr[k]
    ys[...] = total

    def tally_copy(h):
        return remote(ys, yr.at[h], cy_s.at[h], cy_r.at[h], device(lax.rem(y + h, ny), c, z, x))

    for h in range(1, ny):
        tally_copy(h).start()

    lax.fori_loop(nz, nz + ny + nx - 1, round_of, 0)

    for h in range(1, ny):
        tally_copy(h).wait_recv()
        total = total + yr[h]
    factor_out[...] = 2.0 / jnp.maximum(total, 1.0)

    for s in swaps:
        s.wait_send()
    for h in range(1, ny):
        tally_copy(h).wait_send()

    def finish(k, carry):
        @pl.when(k > 0)
        def _():
            z_copy(k).wait_send()
            count_copy(k).wait_send()

        for h in range(ny - 1):
            y_copy(k, h).wait_send()
        for h in range(ny):

            @pl.when(place < nx - 1)
            def _():
                x_copy(k, h).wait_send()

        d_copy(k).wait_send()
        for copy in outs_of(k, xb, c, 0) + outs_of(k, xo, 1 - c, 2) + outs_y(k, yb):
            copy.wait()
        return carry

    lax.fori_loop(0, nz, finish, 0)


def exchange(eff, hid, tok, nz, ny, nx):
    wh, wt = hid.shape[1] // 2, tok.shape[1] // 2
    pairs, tokens = hid.shape[0], tok.shape[0]
    bf, f32 = jnp.bfloat16, jnp.float32
    any_spec = pl.BlockSpec(memory_space=pl.ANY)
    vmem = pl.BlockSpec(memory_space=pltpu.VMEM)
    dma = pltpu.SemaphoreType.DMA
    piece = (nz, ny, ROWS, wh + wt)
    return pl.pallas_call(
        functools.partial(exchange_kernel, nz, ny, nx),
        out_shape=(
            jax.ShapeDtypeStruct((2, nz, ny, ROWS, wh), bf),
            jax.ShapeDtypeStruct((2, nz, ny, ROWS, wt), bf),
            jax.ShapeDtypeStruct((nz, ny, ROWS, wh), bf),
            jax.ShapeDtypeStruct((nz, ny, ROWS, wt), bf),
            jax.ShapeDtypeStruct((8, 128), f32),
        ),
        in_specs=[vmem] * 3,
        out_specs=(any_spec,) * 4 + (vmem,),
        scratch_shapes=[
            pltpu.VMEM((1, pairs), jnp.int32),
            pltpu.VMEM((pairs, wh), bf),
            pltpu.VMEM((tokens, wt), bf),
            pltpu.VMEM((nz, ROWS, wh + wt), bf),
            pltpu.VMEM(piece, bf),
            pltpu.VMEM(piece, bf),
            pltpu.VMEM(piece, bf),
            pltpu.VMEM((nz, 8, 128), f32),
            pltpu.VMEM((nz, 8, 128), f32),
            pltpu.VMEM((8, 128), f32),
            pltpu.VMEM((ny, 8, 128), f32),
            dma((3,)), dma((3,)),
            dma((nz,)), dma((nz,)),
            dma((nz, ny)), dma((nz, ny)),
            dma((nz, ny)), dma((nz, ny)),
            dma((nz,)), dma((nz,)),
            dma((nz,)), dma((nz,)),
            dma((ny,)), dma((ny,)),
            dma((nz, 6)),
        ],
        compiler_params=pltpu.CompilerParams(
            collective_id=0, has_side_effects=True, vmem_limit_bytes=40 * 1024 * 1024
        ),
        cost_estimate=pl.CostEstimate(flops=10**9, bytes_accessed=20 * 2**20, transcendentals=0),
    )(eff, hid, tok)


def on_device(tokens, hidden, routes, lengths):
    nz = lax.axis_size("expert")
    ny = lax.axis_size("dp") // 2
    nx = lax.axis_size("tile")
    token_count, top, width = hidden.shape
    live = jnp.arange(token_count, dtype=jnp.int32) < lengths[0]
    eff = jnp.where(live[None, :], routes.T, nz).reshape(1, top * token_count)
    hid = hidden.transpose(1, 0, 2).reshape(top * token_count, width)
    xh, xt, yh, yt, factor = exchange(eff, hid, tokens, nz, ny, nx)
    rows = nz * ny * ROWS

    def gram(left, right):
        left = left.reshape(2, rows, left.shape[-1])
        right = right.reshape(rows, right.shape[-1])
        out = lax.dot_general(left, right, (((1,), (0,)), ((), ())), preferred_element_type=jnp.float32)
        return (out * factor[0, 0]).reshape(1, 2 * left.shape[-1], right.shape[-1])

    return gram(xt, yt), gram(xh, yh)


def solution(mesh):
    placed = (
        P(("dp", "expert"), "tile"),
        P(("dp", "expert"), None, "tile"),
        P(("dp", "expert"), None),
        P(("dp", "expert")),
    )
    return jax.shard_map(
        on_device,
        mesh=mesh,
        in_specs=placed,
        out_specs=(P("expert", "tile", "dp"), P("expert", "tile", "dp")),
        check_vma=False,
    )
```

time: 227 us -> 99.1 us (0.44); the launches traced: 224 us -> 98.9 us
  waiting for transfers between devices: 112 us -> 0 us
  Pallas kernels: 0 us -> 82 us
  blocking collectives: 48.6 us -> 0 us
  starting transfers between devices: 17.3 us -> 0 us
  between operations: 15.3 us -> 1.3 us
  local copies, waits for them, and re-layouts: 13 us -> 2.59 us
  matrix products: 15.8 us -> 12.3 us
    all_gather x3 -> x0, waiting for transfers between devices: 104 us -> none  [the longest x1 54 us: side_by_side(): lax.all_gather(both, axis, axis=dim, tiled=True)]
    pallas_call x0 -> x1, Pallas kernels: none -> 82 us  [exchange(): pl.pallas_call(functools.partial(exchange_kernel, nz, ny, nx), out_shape=...]
    all_to_all x1 -> x0, blocking collectives: 48.6 us -> none  [sent_together(): lax.all_to_all(both, axis, split_axis=split_dim, concat_axis=concat_dim,...]
    all_to_all x3 -> x0, starting transfers between devices: 17.2 us -> none  [the longest x1 6.67 us: from_everyone(): return lax.all_to_all(copies, axis, split_axis=0, concat_axis=0, tiled=True)]
    all_to_all x4 -> x0, local copies, waits for them, and re-layouts: 7.82 us -> none  [the longest x1 3.69 us: on_device(): lax.all_to_all(full_hidden, 'dp', split_axis=1, concat_axis=0, tiled=True)]
    all_to_all x3 -> x0, waiting for transfers between devices: 7.57 us -> none  [the longest x1 7.56 us: on_device(): lax.all_to_all(full_hidden, 'dp', split_axis=1, concat_axis=0, tiled=True)]
    dot_general x4 -> x2, matrix products: 15.8 us -> 12.3 us  [gram(): lax.dot_general(left, right, (((1,), (0,)), ((), ())), preferred_element_...]
  transfers between devices with their start and end apart: 6 -> 0, of which waited for: 4 -> 0; matrix products, arithmetic and copies ran while one was open for 8% -> 0% of each run, Pallas kernels for 0% -> 0%
where the time goes in v1:
time: 99.1 us; the launch traced here: 98.9 us
  Pallas kernels  82 us (83%)
  matrix products  12.3 us (12%)
  local copies, waits for them, and re-layouts  2.59 us (3%)
  between operations  1.3 us (1%)
    pallas_call x1, Pallas kernels, exchange(): pl.pallas_call(functools.partial(exchange_kernel, nz, ny, nx), out_shape=...  82 us
    dot_general x2, matrix products, gram(): lax.dot_general(left, right, (((1,), (0,)), ((), ())), preferred_element_...  12.3 us

profile of v1, /device:TPU:8, one launch (start us, length us, event | category | flops | bytes accessed | tf_op | source)
XLA Modules:
  0.0 98.9 jit_solution(16934563213944931160)
XLA Ops:
  1.3 0.7 select_bitcast_fusion
  2.0 0.1 reshape.24.eff_ref
  2.1 1.1 %copy.6 = bf16[2,64,1792]{2,1,0:T(8,128)(2,1)S(1)} copy(bf16[2,64,1792]{2,0,1:T(2,128)(2,1)} %bitcast.40) | data formatting | bytes 917504 | tf_op jit(solution)/shard_map/transpose | solution.py:330
  3.1 0.0 copy-start
  3.1 0.9 copy-done
  4.0 82.0 %shard_map.59 = (bf16[2,8,4,48,896]{4,3,2,1,0:T(8,128)(2,1)S(1)}, bf16[2,8,4,48,512]{4,3,2,1,0:T(8,128)(2,1)S(1)}, bf16[8,4,48,896]{3,2,1,0:T(8,128)(2,1)S(1)}, ...) custom-call(s32[1,128]{1,0:T(1,128)S(1)} %reshape.24.eff_ref, bf16[128,1792]{1,0:T(8,128)(2,1)S(1)} %bitcast.39, ...), custom_call_target="tpu_custom_call" | custom-call | flops 1000000000 | bytes 20971520 | tf_op jit(solution)/shard_map/pallas_call | solution.py:284
  86.0 0.5 slice.4
  86.6 3.8 %bitcast_multiply_fusion.1 = f32[2,512,512]{2,1,0:T(8,128)} fusion(bf16[2,8,4,48,512]{4,3,2,1,0:T(8,128)(2,1)S(1)} %get-tuple-element.7, bf16[8,4,48,512]{3,2,1,0:T(8,128)(2,1)S(1)} %get-tuple-element.8, f32[]{:T(128)} %bitcast.8), kind=kOutput, calls=%fused_computation.3 | convolution fusion | flops 1611137024 | bytes 6815748 | tf_op jit(solution)/shard_map/dot_general | solution.py:337
  90.3 8.6 %bitcast_multiply_fusion = f32[2,896,896]{2,1,0:T(8,128)} fusion(f32[]{:T(128)} %bitcast.8, bf16[2,8,4,48,896]{4,3,2,1,0:T(8,128)(2,1)S(1)} %get-tuple-element.10, bf16[8,4,48,896]{3,2,1,0:T(8,128)(2,1)S(1)} %get-tuple-element.11), kind=kOutput, calls=%fused_computation | convolution fusion | flops 4934107136 | bytes 14680068 | tf_op jit(solution)/shard_map/dot_general | solution.py:337
  (1 shorter events, 0.0 us)
Async XLA Ops:
  3.1 0.9 copy-start

commit v2 on v1

v2 whole, which is shorter than its diff:
```python
import functools

import jax
import jax.numpy as jnp
from jax import lax
from jax.experimental import pallas as pl
from jax.experimental.pallas import tpu as pltpu
from jax.sharding import PartitionSpec as P

MESH = pl.DeviceIdType.MESH
CAP = 24
ROWS = 2 * CAP
LAST = 1


def positions(eff, experts, base):
    pairs = eff.shape[1]
    expert = lax.broadcasted_iota(jnp.int32, (experts, pairs), 0)
    hit = jnp.where(eff == expert, 1.0, 0.0)
    earlier = lax.broadcasted_iota(jnp.int32, (pairs, pairs), 0) < lax.broadcasted_iota(
        jnp.int32, (pairs, pairs), 1
    )
    before = jnp.dot(
        hit.astype(jnp.bfloat16),
        jnp.where(earlier, 1.0, 0.0).astype(jnp.bfloat16),
        preferred_element_type=jnp.float32,
    )
    rank = jnp.sum(hit * before, axis=0, keepdims=True).astype(jnp.int32)
    return eff * ROWS + base + rank


def exchange_kernel(
    nz, ny, nx,
    eff_ref, hid_ref, tok_ref,
    xs, yb, acc_h, acc_t, factor_out,
    eff_p, hid_p, tok_p, gath, cs, cr, ys, yr,
    pair_s, pair_r, zs, zr, ysend, yrecv, xsend, xrecv, ds, dr, cz_s, cz_r, cy_s, cy_r, local_sem,
):
    d, z, x = lax.axis_index("dp"), lax.axis_index("expert"), lax.axis_index("tile")
    y, c = d // 2, d % 2
    wh = hid_ref.shape[1] // 2
    wt = tok_ref.shape[1] // 2

    def device(yy, cc, zz, xx):
        return {"dp": yy * 2 + cc, "expert": zz, "tile": xx}

    step = 1 - 2 * c
    y_next = lax.rem(y + step + ny, ny)
    x_next = lax.rem(x + step + nx, nx)
    place = lax.rem((x - y) * step + 2 * nx, nx)
    partner = device(y, 1 - c, z, x)
    to_y, to_x = device(y_next, c, z, x), device(y, c, z, x_next)

    def z_offset(k):
        return lax.rem(jnp.where(k % 2 == 1, (k + 1) // 2, nz - k // 2), nz)

    barrier = pltpu.get_barrier_semaphore()
    for o in range(1, nz):
        pl.semaphore_signal(barrier, inc=1, device_id=device(y, c, lax.rem(z + o, nz), x), device_id_type=MESH)
    for o in range(1, ny):
        pl.semaphore_signal(barrier, inc=1, device_id=device(lax.rem(y + o, ny), c, z, x), device_id_type=MESH)
    for o in (1, nx - 1):
        pl.semaphore_signal(barrier, inc=1, device_id=device(y, c, z, lax.rem(x + o, nx)), device_id_type=MESH)
    pl.semaphore_signal(barrier, inc=1, device_id=partner, device_id_type=MESH)

    def remote(src, dst, s, r, to):
        return pltpu.make_async_remote_copy(
            src_ref=src, dst_ref=dst, send_sem=s, recv_sem=r, device_id=to, device_id_type=MESH
        )

    theirs_h = pl.ds(pl.multiple_of((1 - c) * wh, 128), wh)
    theirs_t = pl.ds(pl.multiple_of((1 - c) * wt, 128), wt)
    swaps = (
        remote(eff_ref, eff_p, pair_s.at[0], pair_r.at[0], partner),
        remote(hid_ref.at[:, theirs_h], hid_p, pair_s.at[1], pair_r.at[1], partner),
        remote(tok_ref.at[:, theirs_t], tok_p, pair_s.at[2], pair_r.at[2], partner),
    )
    pl.semaphore_wait(barrier, nz - 1 + ny - 1 + 2 + 1)
    for s in swaps:
        s.start()
    eff_mine = eff_ref[...]
    mine_h = hid_ref[:, pl.ds(pl.multiple_of(c * wh, 128), wh)]
    mine_t = tok_ref[:, pl.ds(pl.multiple_of(c * wt, 128), wt)]
    mine_t2 = jnp.concatenate([mine_t, mine_t], axis=0)
    slot_mine = positions(eff_mine, nz, c * CAP)
    for s in swaps:
        s.wait_recv()
    eff_theirs = eff_p[...]
    slot_theirs = positions(eff_theirs, nz, (1 - c) * CAP)
    pairs = eff_mine.shape[1]

    def gathered(e, out):
        slot = lax.broadcasted_iota(jnp.int32, (ROWS, pairs), 0) + e * ROWS
        a = jnp.where(slot == slot_mine, 1.0, 0.0).astype(jnp.bfloat16)
        b = jnp.where(slot == slot_theirs, 1.0, 0.0).astype(jnp.bfloat16)
        their_t = tok_p[...]
        out[:, :wh] = (
            jnp.dot(a, mine_h, preferred_element_type=jnp.float32)
            + jnp.dot(b, hid_p[...], preferred_element_type=jnp.float32)
        ).astype(jnp.bfloat16)
        out[:, wh:] = (
            jnp.dot(a, mine_t2, preferred_element_type=jnp.float32)
            + jnp.dot(b, jnp.concatenate([their_t, their_t], axis=0), preferred_element_type=jnp.float32)
        ).astype(jnp.bfloat16)

    def tally(e):
        hits = jnp.where(eff_mine == e, 1.0, 0.0) + jnp.where(eff_theirs == e, 1.0, 0.0)
        return jnp.broadcast_to(jnp.sum(hits, axis=1, keepdims=True), (8, 128))

    def z_copy(k):
        to = device(y, c, lax.rem(z + nz - z_offset(k), nz), x)
        return remote(gath.at[k], xs.at[c, k, y], zs.at[k], zr.at[k], to)

    def count_copy(k):
        to = device(y, c, lax.rem(z + nz - z_offset(k), nz), x)
        return remote(cs.at[k], cr.at[k], cz_s.at[k], cz_r.at[k], to)

    def row_of(h):
        return lax.rem(y + ny * h - h * step, ny)

    def y_copy(k, h):
        here = xs.at[c, k, row_of(h)]
        return remote(here, here, ysend.at[k, h], yrecv.at[k, h + 1], to_y)

    def y_arrival(k, h):
        here = xs.at[c, k, row_of(h)]
        return remote(here, here, ysend.at[k, h - 1], yrecv.at[k, h], to_y)

    def x_first(k, h):
        yy = row_of(h)
        return remote(xs.at[c, k, yy], yb.at[k, yy], xsend.at[k, h], xrecv.at[k, h], to_x)

    def x_copy(k, h):
        here = yb.at[k, row_of(h)]
        return remote(here, here, xsend.at[k, h], xrecv.at[k, h], to_x)

    def d_copy(k):
        return remote(xs.at[c, k], xs.at[c, k], ds.at[k], dr.at[k], partner)

    def d_arrival(k):
        return remote(xs.at[1 - c, k], xs.at[1 - c, k], ds.at[k], dr.at[k], partner)

    def columns_copy(k):
        return pltpu.make_async_copy(xs.at[c, k], yb.at[k], local_sem.at[k])

    def first_step(k):
        y_copy(k, 0).start()

        @pl.when(place == 0)
        def _():
            x_first(k, 0).start()

    gathered(z, xs.at[c, 0, y])
    first_step(0)

    def fill(k, carry):
        e = lax.rem(z + nz - z_offset(k), nz)
        gathered(e, gath.at[k])
        z_copy(k).start()
        cs[k] = tally(e)
        count_copy(k).start()
        return carry

    lax.fori_loop(1, nz, fill, 0)

    def add_product(k, half, lo, size, acc, first, width, row):
        left = xs[half, k, :, :, lo : lo + size].reshape(ny * ROWS, size)
        right = yb[k, :, :, first : first + width].reshape(ny * ROWS, width)
        part = lax.dot_general(left, right, (((0,), (0,)), ((), ())), preferred_element_type=jnp.float32)
        rows = pl.ds(row, size)

        @pl.when(k == 0)
        def _():
            acc[rows, :] = part

        @pl.when(k > 0)
        def _():
            acc[rows, :] += part

    def product(k, half, part):
        tiles = hidden_tiles(wh)
        if part < len(tiles):
            lo, size = tiles[part]
            add_product(k, half, lo, size, acc_h, 0, wh, half * wh + lo)
        else:
            add_product(k, half, wh, wt, acc_t, wh, wt, half * wt)

    parts = len(hidden_tiles(wh)) + 1

    def round_of(i, carry):
        k_dot = i - ny - place
        dot_now = (k_dot >= 0) & (k_dot < nz - LAST)

        @pl.when(i < nz)
        def _():
            z_copy(i).wait_recv()
            first_step(i)

        for h in range(1, ny):
            k = i - h

            @pl.when((k >= 0) & (k < nz))
            def _():
                y_arrival(k, h).wait_recv()
                if h < ny - 1:
                    y_copy(k, h).start()

                @pl.when(place == 0)
                def _():
                    x_first(k, h).start()

                if h == ny - 1:
                    d_copy(k).start()

                    @pl.when(place == 0)
                    def _():
                        columns_copy(k).start()

            if h == 1:

                @pl.when(dot_now)
                def _():
                    d_arrival(k_dot).wait_recv()

                    @pl.when(place == 0)
                    def _():
                        columns_copy(k_dot).wait()

                    for part in range(parts):
                        product(k_dot, 0, part)

        @pl.when(i == nz - 1)
        def _():
            total = tally(z)
            for k in range(1, nz):
                count_copy(k).wait_recv()
                total = total + cr[k]
            ys[...] = total
            for h in range(1, ny):
                tally_copy(h).start()

        for h in range(ny):
            k = i - place - h

            @pl.when((place > 0) & (k >= 0) & (k < nz))
            def _():
                x_first(k, h).wait_recv()

                @pl.when(place < nx - 1)
                def _():
                    x_copy(k, h).start()

            if h == 1:

                @pl.when(dot_now)
                def _():
                    for part in range(parts):
                        product(k_dot, 1, part)

        return carry

    def tally_copy(h):
        return remote(ys, yr.at[h], cy_s.at[h], cy_r.at[h], device(lax.rem(y + h, ny), c, z, x))

    lax.fori_loop(1, nz + ny + nx - 2, round_of, 0)

    total = ys[...]
    for h in range(1, ny):
        tally_copy(h).wait_recv()
        total = total + yr[h]
    factor_out[...] = 2.0 / jnp.maximum(total, 1.0)

    for k in range(nz - LAST, nz):
        d_arrival(k).wait_recv()

        @pl.when(place == 0)
        def _():
            columns_copy(k).wait()

    for s in swaps:
        s.wait_send()
    for h in range(1, ny):
        tally_copy(h).wait_send()

    def finish(k, carry):
        @pl.when(k > 0)
        def _():
            z_copy(k).wait_send()
            count_copy(k).wait_send()

        for h in range(ny - 1):
            y_copy(k, h).wait_send()
        for h in range(ny):

            @pl.when(place < nx - 1)
            def _():
                x_copy(k, h).wait_send()

        d_copy(k).wait_send()
        return carry

    lax.fori_loop(0, nz, finish, 0)


def hidden_tiles(width):
    half = width // 256 * 128
    return ((0, half), (half, width - half)) if half else ((0, width),)


def exchange(eff, hid, tok, nz, ny, nx):
    wh, wt = hid.shape[1] // 2, tok.shape[1] // 2
    pairs, tokens = hid.shape[0], tok.shape[0]
    bf, f32 = jnp.bfloat16, jnp.float32
    vmem = pl.BlockSpec(memory_space=pltpu.VMEM)
    dma = pltpu.SemaphoreType.DMA
    piece = (nz, ny, ROWS, wh + wt)
    return pl.pallas_call(
        functools.partial(exchange_kernel, nz, ny, nx),
        out_shape=(
            jax.ShapeDtypeStruct((2, *piece), bf),
            jax.ShapeDtypeStruct(piece, bf),
            jax.ShapeDtypeStruct((2 * wh, wh), f32),
            jax.ShapeDtypeStruct((2 * wt, wt), f32),
            jax.ShapeDtypeStruct((8, 128), f32),
        ),
        in_specs=[vmem] * 3,
        out_specs=(vmem,) * 5,
        scratch_shapes=[
            pltpu.VMEM((1, pairs), jnp.int32),
            pltpu.VMEM((pairs, wh), bf),
            pltpu.VMEM((tokens, wt), bf),
            pltpu.VMEM((nz, ROWS, wh + wt), bf),
            pltpu.VMEM((nz, 8, 128), f32),
            pltpu.VMEM((nz, 8, 128), f32),
            pltpu.VMEM((8, 128), f32),
            pltpu.VMEM((ny, 8, 128), f32),
            dma((3,)), dma((3,)),
            dma((nz,)), dma((nz,)),
            dma((nz, ny)), dma((nz, ny)),
            dma((nz, ny)), dma((nz, ny)),
            dma((nz,)), dma((nz,)),
            dma((nz,)), dma((nz,)),
            dma((ny,)), dma((ny,)),
            dma((nz,)),
        ],
        compiler_params=pltpu.CompilerParams(
            collective_id=0, has_side_effects=True, vmem_limit_bytes=12 * 1024 * 1024
        ),
        cost_estimate=pl.CostEstimate(flops=6 * 10**9, bytes_accessed=20 * 2**20, transcendentals=0),
    )(eff, hid, tok)


def finish_kernel(nz, xs, yb, acc_h, acc_t, factor_ref, out_h, out_t, res_h, res_t, sem):
    ny = xs.shape[2]
    wh, wt = acc_h.shape[1], acc_t.shape[1]
    depth = LAST * ny * ROWS
    factor = factor_ref[0:1, 0:1]
    copies = []
    for half in range(2):
        tiles = [(lo, size, half * wh + lo, acc_h, res_h, out_h, 0, wh) for lo, size in hidden_tiles(wh)]
        tiles.append((wh, wt, half * wt, acc_t, res_t, out_t, wh, wh + wt))
        for lo, size, row, acc, res, out, first, last in tiles:
            left = xs[half, nz - LAST :, :, :, lo : lo + size].reshape(depth, size)
            right = yb[nz - LAST :, :, :, first:last].reshape(depth, last - first)
            part = lax.dot_general(left, right, (((0,), (0,)), ((), ())), preferred_element_type=jnp.float32)
            res[row : row + size, :] = (acc[row : row + size, :] + part) * factor
            copy = pltpu.make_async_copy(
                res.at[pl.ds(row, size), :], out.at[0, pl.ds(row, size), :], sem.at[len(copies)]
            )
            copy.start()
            copies.append(copy)
    for copy in copies:
        copy.wait()


def finish(xs, yb, acc_h, acc_t, factor, nz):
    f32 = jnp.float32
    any_spec = pl.BlockSpec(memory_space=pl.ANY)
    vmem = pl.BlockSpec(memory_space=pltpu.VMEM)
    return pl.pallas_call(
        functools.partial(finish_kernel, nz),
        out_shape=(
            jax.ShapeDtypeStruct((1, *acc_h.shape), f32),
            jax.ShapeDtypeStruct((1, *acc_t.shape), f32),
        ),
        in_specs=[vmem] * 5,
        out_specs=(any_spec, any_spec),
        scratch_shapes=[
            pltpu.VMEM(acc_h.shape, f32),
            pltpu.VMEM(acc_t.shape, f32),
            pltpu.SemaphoreType.DMA((2 * len(hidden_tiles(acc_h.shape[1])) + 2,)),
        ],
        compiler_params=pltpu.CompilerParams(vmem_limit_bytes=12 * 1024 * 1024),
        cost_estimate=pl.CostEstimate(flops=10**9, bytes_accessed=9 * 2**20, transcendentals=0),
    )(xs, yb, acc_h, acc_t, factor)


def on_device(tokens, hidden, routes, lengths):
    nz = lax.axis_size("expert")
    ny = lax.axis_size("dp") // 2
    nx = lax.axis_size("tile")
    token_count, top, width = hidden.shape
    live = jnp.arange(token_count, dtype=jnp.int32) < lengths[0]
    eff = jnp.where(live[None, :], routes.T, nz).reshape(1, top * token_count)
    hid = hidden.transpose(1, 0, 2).reshape(top * token_count, width)
    xs, yb, acc_h, acc_t, factor = exchange(eff, hid, tokens, nz, ny, nx)
    down, into = finish(xs, yb, acc_h, acc_t, factor, nz)
    return into, down


def solution(mesh):
    placed = (
        P(("dp", "expert"), "tile"),
        P(("dp", "expert"), None, "tile"),
        P(("dp", "expert"), None),
        P(("dp", "expert")),
    )
    return jax.shard_map(
        on_device,
        mesh=mesh,
        in_specs=placed,
        out_specs=(P("expert", "tile", "dp"), P("expert", "tile", "dp")),
        check_vma=False,
    )
```

time: 99.1 us -> 88.7 us (0.90)
  matrix products: 12.3 us -> 0 us
  Pallas kernels: 82 us -> 84.5 us
    dot_general x2 -> x0, matrix products: 12.3 us -> none  [gram(): lax.dot_general(left, right, (((1,), (0,)), ((), ())), preferred_element_...]
    pallas_call x0 -> x1, Pallas kernels: none -> 3.8 us  [finish(): pl.pallas_call(functools.partial(finish_kernel, nz), out_shape=(jax.Shape...]
    pallas_call x1, Pallas kernels: 82 us -> 80.7 us  [exchange(): pl.pallas_call(functools.partial(exchange_kernel, nz, ny, nx), out_shape=...]
where the time goes in v2:
time: 88.7 us; the launch traced here: 88.5 us
  Pallas kernels  84.5 us (95%)
  local copies, waits for them, and re-layouts  2.05 us (2%)
  between operations  1.3 us (1%)
    pallas_call x1, Pallas kernels, exchange(): pl.pallas_call(functools.partial(exchange_kernel, nz, ny, nx), out_shape=...  80.7 us
    pallas_call x1, Pallas kernels, finish(): pl.pallas_call(functools.partial(finish_kernel, nz), out_shape=(jax.Shape...  3.8 us

profile of v2, /device:TPU:8, one launch (start us, length us, event | category | flops | bytes accessed | tf_op | source)
XLA Modules:
  0.0 88.5 jit_solution(643740499731151227)
XLA Ops:
  1.3 0.7 select_bitcast_fusion
  2.0 0.1 reshape.14.eff_ref
  2.1 1.1 %copy.6 = bf16[2,64,1792]{2,1,0:T(8,128)(2,1)S(1)} copy(bf16[2,64,1792]{2,0,1:T(2,128)(2,1)} %bitcast.7) | data formatting | bytes 917504 | tf_op jit(solution)/shard_map/transpose | solution.py:405
  3.1 0.0 copy-start
  3.1 0.9 %copy-done = bf16[64,1024]{1,0:T(8,128)(2,1)S(1)} copy-done((bf16[64,1024]{1,0:T(8,128)(2,1)S(1)}, bf16[64,1024]{1,0:T(8,128)(2,1)}, u32[]{:S(2)}) %copy-start) | copy-done | bytes 131096
  4.0 80.7 %shard_map.59 = (bf16[2,8,4,48,1408]{4,3,2,1,0:T(8,128)(2,1)S(1)}, bf16[8,4,48,1408]{3,2,1,0:T(8,128)(2,1)S(1)}, f32[1792,896]{1,0:T(8,128)S(1)}, f32[1024,512]{1,0:T(8,128)S(1)}, f32[8,128]{1,0:T(8,128)S(1)}) custom-call(s32[1,128]{1,0:T(1,128)S(1)} %reshape.14.eff_ref, bf16[128,1792]{1,0:T(8,128)(2,1)S(1)} %bitcast.6, bf16[64,1024]{1,0:T(8,128)(2,1)S(1)} %copy-done), custom_call_target="tpu_custom_call" | custom-call | flops 6000000000 | bytes 20971520 | tf_op jit(solution)/shard_map/pallas_call | solution.py:317
  84.7 3.8 %shard_map.60 = (f32[1,1792,896]{2,1,0:T(8,128)}, f32[1,1024,512]{2,1,0:T(8,128)}) custom-call(bf16[2,8,4,48,1408]{4,3,2,1,0:T(8,128)(2,1)S(1)} %get-tuple-element.9.xs, bf16[8,4,48,1408]{3,2,1,0:T(8,128)(2,1)S(1)} %get-tuple-element.10.yb, f32[1792,896]{1,0:T(8,128)S(1)} %get-tuple-element.11.acc_h, f32[1024,512]{1,0:T(8,128)S(1)} %get-tuple-element.12.acc_t, ...), custom_call_target="tpu_custom_call" | custom-call | flops 1000000000 | bytes 9437184 | tf_op jit(solution)/shard_map/pallas_call | solution.py:380
  (1 shorter events, 0.0 us)
Async XLA Ops:
  3.1 0.9 %copy-start = (bf16[64,1024]{1,0:T(8,128)(2,1)S(1)}, bf16[64,1024]{1,0:T(8,128)(2,1)}, u32[]{:S(2)}) copy-start(bf16[64,1024]{1,0:T(8,128)(2,1)} %tok_ref.1) | copy-start | bytes 393220
